TPU v7x, 32 devices: a whole 2x2x4 slice. The times are simulated.
32 devices in a mesh: patch: 32 (over z, y, x, core).
Axes of the slice: x: 2, y: 2, z: 4, core: 2. Of those that a mesh axis runs over, the one named last changes fastest.
Arguments:
- atm_flux: bfloat16 [8, 98304], P(None, 'patch'), may hold values from -6 to 6
- remap_send: int32 [32, 5, 8], P('patch'), may hold values from 0 to 23
- remap_target: int32 [32, 5, 8], P('patch'), may hold values from 0 to 31
- remap_counts: int32 [32, 5], P('patch'), may hold values from 0 to 8, as said below
- remap_weights: bfloat16 [32, 5, 8, 128, 128], P('patch'), may hold values from -0.5 to 0.5
- coupling: float32 [2, 8], replicated, may hold values from -2 to 2
- tracer: float32 [2, 128, 131072], P(None, None, 'patch'), may hold values from -6 to 6
- wet: int32 [131072], P('patch'), may hold values from 0 to 1
- mix_inverse: float32 [1024, 128, 128], P('patch')
- halo_send: int32 [32, 4, 2, 128], P('patch'), may hold values from 0 to 4095
- halo_ghost: int32 [32, 4, 2, 128], P('patch'), may hold values from 0 to 4095
- halo_rows: int32 [32, 4], P('patch'), may hold values from 0 to 2, as said below
Outputs:
- ocean_flux: float32 [8, 131072], P(None, 'patch')
- tracer_out: float32 [2, 128, 131072], P(None, None, 'patch')
Inputs may be any that keep to these rules, and one draw needn't show every extreme that they name: `remap_counts`: some entry equals 8. `halo_rows`: some entry equals 2.
All inputs are finite; a program needn't handle non-finite values.
Results may differ from a plain program's by a relative error of at most 0.0003.
Values may be sent and summed in bfloat16 or wider, within the bound.
A program may use at most 64 MiB of HBM per device.

v0:
```python
import jax
import jax.numpy as jnp
from jax import lax
from jax.sharding import PartitionSpec as P


def shifted(array, axis, by):
    length = lax.axis_size(axis)
    return lax.ppermute(array, axis, [(i, (i + by) % length) for i in range(length)])


def route_fluxes(outgoing, offsets):
    pieces = [shifted(outgoing[index], "patch", offsets[index]) for index in range(len(offsets))]
    return jnp.stack(pieces)


def route_halo(outgoing, offsets):
    pieces = [shifted(outgoing[index], "patch", offsets[index]) for index in range(len(offsets))]
    return jnp.stack(pieces)


def body(
    atm_flux,
    remap_send,
    remap_target,
    remap_counts,
    remap_weights,
    coupling,
    tracer,
    wet,
    mix_inverse,
    halo_send,
    halo_ghost,
    halo_rows,
):
    offset_count = remap_send.shape[1]
    radius = offset_count // 2
    capacity = remap_send.shape[2]
    block_cells = remap_weights.shape[-1]
    flux_count = atm_flux.shape[0]
    tracers, levels, ocean_cells = tracer.shape
    ocean_blocks = ocean_cells // block_cells
    atm_blocks = atm_flux.shape[1] // block_cells
    wetf = wet.astype(jnp.float32)
    blocks = atm_flux.reshape(flux_count, atm_blocks, block_cells)
    chooser = (
        remap_send[0].reshape(-1)[:, None] == jnp.arange(atm_blocks, dtype=jnp.int32)[None, :]
    ).astype(jnp.bfloat16)
    selected = jnp.einsum(
        "sa,fab->sfb", chooser, blocks, preferred_element_type=jnp.float32
    ).astype(jnp.bfloat16)
    outgoing = selected.reshape(offset_count, capacity, flux_count, block_cells)
    flux_offsets = [index - radius for index in range(offset_count)]
    arrived = route_fluxes(outgoing, flux_offsets)
    in_use = (jnp.arange(capacity, dtype=jnp.int32)[None, :] < remap_counts[0][:, None]).astype(
        jnp.float32
    )
    contrib = jnp.einsum(
        "dcfi,dcij->dcfj", arrived, remap_weights[0], preferred_element_type=jnp.float32
    )
    contrib = contrib * in_use[:, :, None, None]
    table = (remap_target[0][..., None] == jnp.arange(ocean_blocks, dtype=jnp.int32)).astype(
        jnp.float32
    )
    ocean_flux = (
        jnp.einsum("dcb,dcfj->fbj", table, contrib, precision=lax.Precision.HIGHEST).reshape(
            flux_count, ocean_cells
        )
        * wetf
    )
    surface = jnp.dot(coupling, ocean_flux, precision=lax.Precision.HIGHEST)
    rhs = jnp.concatenate([tracer[:, 0:1, :] + surface[:, None, :], tracer[:, 1:, :]], axis=1)
    shaped = rhs.reshape(tracers, levels, ocean_blocks, block_cells)
    solved = jnp.einsum(
        "blk,tkbc->tlbc", mix_inverse, shaped, precision=lax.Precision.HIGHEST
    ).reshape(tracers, levels, ocean_cells)
    mixed = wetf * solved + (1.0 - wetf) * tracer
    sent = mixed.astype(jnp.bfloat16)
    halo_count = halo_send.shape[1]
    halo_depth = halo_send.shape[2]
    lanes = halo_send.shape[3]
    picks = halo_count * halo_depth * lanes
    cell_ids = jnp.arange(ocean_cells, dtype=jnp.int32)
    source_table = (cell_ids[:, None] == halo_send[0].reshape(-1)[None, :]).astype(jnp.bfloat16)
    gathered = jnp.dot(
        sent.reshape(tracers * levels, ocean_cells),
        source_table,
        preferred_element_type=jnp.float32,
    ).astype(jnp.bfloat16)
    gathered = gathered.reshape(tracers, levels, halo_count, halo_depth, lanes)
    halo_offsets = [index - radius for index in range(radius)] + [
        index + 1 for index in range(radius)
    ]
    halo_out = jnp.transpose(gathered, (2, 3, 0, 1, 4))
    received = route_halo(halo_out, halo_offsets)
    values = (
        jnp.transpose(received, (2, 3, 0, 1, 4))
        .reshape(tracers * levels, picks)
        .astype(jnp.float32)
    )
    ghost_table = (halo_ghost[0].reshape(-1)[:, None] == cell_ids[None, :]).astype(jnp.float32)
    flat_mixed = mixed.reshape(tracers * levels, ocean_cells)
    current = lax.dot_general(
        flat_mixed, ghost_table, (((1,), (1,)), ((), ())), precision=lax.Precision.HIGHEST
    )
    ghost_wet = jnp.dot(ghost_table, wetf, precision=lax.Precision.HIGHEST)
    rows_used = (jnp.arange(halo_depth, dtype=jnp.int32)[None, :] < halo_rows[0][:, None]).astype(
        jnp.float32
    )
    weight = (
        jnp.broadcast_to(rows_used[:, :, None], (halo_count, halo_depth, lanes)).reshape(-1)
        * ghost_wet
    )
    increment = 0.25 * (values - current) * weight[None, :]
    added = jnp.dot(increment, ghost_table, precision=lax.Precision.HIGHEST)
    tracer_out = (flat_mixed + added).reshape(tracers, levels, ocean_cells)
    return (ocean_flux, tracer_out)


def solution(mesh):
    return jax.shard_map(
        body,
        mesh=mesh,
        in_specs=(
            P(None, "patch"),
            P("patch", None, None),
            P("patch", None, None),
            P("patch", None),
            P("patch", None, None, None, None),
            P(),
            P(None, None, "patch"),
            P("patch"),
            P("patch", None, None),
            P("patch", None, None, None),
            P("patch", None, None, None),
            P("patch", None),
        ),
        out_specs=(P(None, "patch"), P(None, None, "patch")),
        check_vma=False,
    )
```

profile of v0, /device:TPU:0, one launch (start us, length us, event | category | flops | bytes accessed | tf_op | source)
XLA Modules:
  0.0 113.3 jit_solution(16242526582116591750)
XLA Ops:
  0.7 0.8 reduce
  1.6 1.0 convolution_convert_fusion
  2.6 7.0 %collective-permute-start = (bf16[8,8,128]{2,0,1:T(8,128)(2,1)S(1)}, bf16[8,8,128]{2,0,1:T(8,128)(2,1)S(1)}, u32[]{:S(2)}, u32[]{:S(2)}) collective-permute-start(bf16[8,8,128]{2,0,1:T(8,128)(2,1)S(1)} %get-tuple-element.12), channel_id=1, source_target_pairs={{0,30},{1,31},{2,0},{3,1},{4,2},{5,3},{6,4},{7,5},{8,6},{9,7},{10,... | collective-permute-start | bytes 49160 | tf_op jit(solution)/shard_map/ppermute | solution.py:9
  9.6 0.5 collective-permute-start.3
  10.2 0.7 collective-permute-start.4
  10.8 0.7 convert_element_type.41
  11.5 0.7 broadcast_subtract_fusion
  12.3 0.7 fusion.34
  13.0 8.2 %fusion.1 = f32[1,1024]{1,0:T(1,128)S(1)} fusion(f32[4096,1]{0,1:T(1,128)S(1)} %bitcast.96, s32[1024]{0:T(1024)} %bitcast.108), kind=kOutput, calls=%fused_computation.2 | convolution fusion | flops 54525952 | bytes 24576 | tf_op jit(solution)/shard_map/dot_general | solution.py:106
  21.3 1.0 slice.43
  22.3 5.8 %copy.36 = f32[2,128,4096]{1,2,0:T(8,128)} copy(f32[2,128,4096]{2,1,0:T(8,128)} %param.18) | data formatting | bytes 8388608 | tf_op args[6]
  28.1 5.4 %slice.54 = f32[2,127,4096]{1,2,0:T(8,128)} slice(f32[2,128,4096]{1,2,0:T(8,128)} %copy.36), slice={[0:2], [1:128], [0:4096]} | slice | bytes 8323072 | tf_op jit(solution)/shard_map/slice | solution.py:72
  33.6 0.4 fusion.22
  34.7 2.7 %copy.37 = f32[2,1,4096]{1,2,0:T(8,128)} copy(f32[2,1,4096]{2,0,1:T(2,128)S(1)} %fusion.9) | data formatting | bytes 65536 | tf_op jit(solution)/shard_map/add | solution.py:72
  37.4 4.6 %pad_maximum_fusion = f32[2,128,4096]{1,2,0:T(8,128)S(1)} fusion(f32[2,127,4096]{1,2,0:T(8,128)} %slice.54, f32[2,1,4096]{1,2,0:T(8,128)} %copy.37), kind=kLoop, calls=%fused_computation.13 | loop fusion | flops 1048576 | bytes 8388608 | tf_op jit(solution)/shard_map/concatenate | solution.py:72
  42.1 4.5 %fusion.13 = f32[2,128,32,128]{1,3,0,2:T(8,128)S(1)} fusion(f32[2,128,32,128]{1,3,2,0:T(8,128)S(1)} %bitcast.91, f32[32,128,128]{2,1,0:T(8,128)S(1)} %copy-done), kind=kOutput, calls=%fused_computation.18 | convolution fusion | flops 1610612736 | bytes 10485760 | tf_op jit(solution)/shard_map/blk,tkbc->tlbc/dot_general | solution.py:74
  46.8 1.9 %copy-done.1 = f32[2,128,4096]{1,2,0:T(8,128)S(1)} copy-done((f32[2,128,4096]{1,2,0:T(8,128)S(1)}, f32[2,128,4096]{1,2,0:T(8,128)}, u32[]{:S(2)}) %copy-start.1) | copy-done | bytes 4194328
  48.7 4.1 %fusion.36 = (bf16[2,128,4096]{1,2,0:T(8,128)(2,1)}, f32[2,128,4096]{1,2,0:T(8,128)}) fusion(f32[2,128,4096]{1,2,0:T(8,128)S(1)} %copy-done.1, f32[4096]{0:T(1024)S(1)} %broadcast_subtract_fusion, f32[2,128,32,128]{1,3,2,0:T(8,128)S(1)} %copy.39, f32[4096]{0:T(1024)S(1)} %convert_element_type.41), kind=kLoop, calls=%fused_computation.56 | loop fusion | flops 4194304 | bytes 14712832 | tf_op jit(solution)/shard_map/convert_element_type | solution.py:78
  52.8 4.2 %copy.42 = bf16[2,128,4096]{2,1,0:T(8,128)(2,1)} copy(bf16[2,128,4096]{1,2,0:T(8,128)(2,1)} %get-tuple-element.2) | data formatting | bytes 4194304 | tf_op jit(solution)/shard_map/convert_element_type | solution.py:78
  57.0 4.9 %fusion.21 = bf16[256,1024]{1,0:T(8,128)(2,1)S(1)} fusion(bf16[256,4096]{1,0:T(8,128)(2,1)} %bitcast.94, s32[1024]{0:T(1024)S(1)} %bitcast.107), kind=kOutput, calls=%fused_computation.24 | convolution fusion | flops 2151940096 | bytes 2625536 | tf_op jit(solution)/shard_map/dot_general | solution.py:85
  61.9 0.4 reshape.109
  63.0 5.0 %collective-permute-start.5 = (bf16[2,2,128,128]{3,0,2,1:T(2,128)(2,1)S(1)}, bf16[2,2,128,128]{3,0,2,1:T(2,128)(2,1)S(1)}, u32[]{:S(2)}, u32[]{:S(2)}) collective-permute-start(bf16[2,2,128,128]{3,0,2,1:T(2,128)(2,1)S(1)} %get-tuple-element.4), channel_id=1, source_target_pairs={{0,30},{1,31},{2,0},{3,1},{4,2},{5,3},{6,4},{7,5},{8,6},{9,7},{10,... | collective-permute-start | bytes 393224 | tf_op jit(solution)/shard_map/ppermute | solution.py:9
  68.0 0.7 collective-permute-start.6
  68.7 1.2 %collective-permute-start.8 = (bf16[2,2,128,128]{3,0,2,1:T(2,128)(2,1)S(1)}, bf16[2,2,128,128]{3,0,2,1:T(2,128)(2,1)S(1)}, u32[]{:S(2)}, u32[]{:S(2)}) collective-permute-start(bf16[2,2,128,128]{3,0,2,1:T(2,128)(2,1)S(1)} %get-tuple-element.5), channel_id=1, source_target_pairs={{0,2},{1,3},{2,4},{3,5},{4,6},{5,7},{6,8},{7,9},{8,10},{9,11},{10,... | collective-permute-start | bytes 393224 | tf_op jit(solution)/shard_map/ppermute | solution.py:9
  70.0 5.6 %copy.41 = f32[2,128,4096]{2,1,0:T(8,128)} copy(f32[2,128,4096]{1,2,0:T(8,128)} %get-tuple-element.3) | data formatting | bytes 8388608 | tf_op jit(solution)/shard_map/add | solution.py:77
  75.6 1.9 %collective-permute-done.7 = bf16[2,2,128,128]{3,0,2,1:T(2,128)(2,1)S(1)} collective-permute-done((bf16[2,2,128,128]{3,0,2,1:T(2,128)(2,1)S(1)}, bf16[2,2,128,128]{3,0,2,1:T(2,128)(2,1)S(1)}, u32[]{:S(2)}, u32[]{:S(2)}) %collective-permute-start.7) | collective-permute-done | bytes 131104 | tf_op jit(solution)/shard_map/ppermute | solution.py:9
  77.5 1.2 %collective-permute-done.8 = bf16[2,2,128,128]{3,0,2,1:T(2,128)(2,1)S(1)} collective-permute-done((bf16[2,2,128,128]{3,0,2,1:T(2,128)(2,1)S(1)}, bf16[2,2,128,128]{3,0,2,1:T(2,128)(2,1)S(1)}, u32[]{:S(2)}, u32[]{:S(2)}) %collective-permute-start.8) | collective-permute-done | bytes 131104 | tf_op jit(solution)/shard_map/ppermute | solution.py:9
  78.7 0.7 copy-done.5
  79.3 1.6 %convert_bitcast_fusion = f32[2,128,4,2,128]{4,3,2,1,0:T(2,128)S(1)} fusion(bf16[1,2,2,128,128]{4,1,0,3,2:T(2,128)(2,1)} %bitcast.100, bf16[1,2,2,128,128]{4,1,0,3,2:T(2,128)(2,1)S(1)} %bitcast.99, bf16[1,2,2,128,128]{4,1,0,3,2:T(2,128)(2,1)S(1)} %bitcast.98, bf16[1,2,2,128,128]{4,1,0,3,2:T(2,128)(2,1)S(1)} %bitcast.97), kind=kLoop, calls=%fused_computation.28 | loop fusion | flops 1048576 | bytes 1572864 | tf_op jit(solution)/shard_map/convert_element_type | solution.py:99
  81.0 1.8 %reshape.112 = f32[256,1024]{1,0:T(8,128)} reshape(f32[2,128,4,2,128]{4,3,2,1,0:T(2,128)S(1)} %convert_bitcast_fusion) | data formatting | bytes 2097152 | tf_op jit(solution)/shard_map/convert_element_type | solution.py:99
  82.8 20.4 %fusion.20 = f32[256,1024]{1,0:T(8,128)S(1)} fusion(f32[256,1024]{1,0:T(8,128)} %reshape.112, f32[256,4096]{1,0:T(8,128)} %bitcast.92, s32[1024]{0:T(1024)S(1)} %bitcast.109, f32[1024]{0:T(1024)S(1)} %multiply_multiply_fusion), kind=kOutput, calls=%fused_computation.23 | convolution fusion | flops 12889620480 | bytes 6299648 | tf_op jit(solution)/shard_map/dot_general | solution.py:103
  103.2 10.1 %fusion.8 = f32[256,4096]{1,0:T(8,128)} fusion(f32[256,4096]{1,0:T(8,128)S(1)} %bitcast.93, f32[256,1024]{1,0:T(8,128)S(1)} %fusion.20, s32[1024]{0:T(1024)S(1)} %bitcast.110), kind=kOutput, calls=%fused_computation.10 | convolution fusion | flops 12890144768 | bytes 9441280 | tf_op jit(solution)/shard_map/dot_general | solution.py:115
  (47 shorter events, 2.0 us)
Async XLA Ops:
  0.6 41.4 %copy-start = (f32[32,128,128]{2,1,0:T(8,128)S(1)}, f32[32,128,128]{2,1,0:T(8,128)}, u32[]{:S(2)}) copy-start(f32[32,128,128]{2,1,0:T(8,128)} %param.20) | copy-start | bytes 6291460
  0.6 20.6 %copy-start.8 = (s32[1,4]{1,0:T(1,128)S(1)}, s32[1,4]{1,0:T(1,128)}, u32[]{:S(2)}) copy-start(s32[1,4]{1,0:T(1,128)} %param.23) | copy-start | bytes 52
  2.6 30.9 %collective-permute-start = (bf16[8,8,128]{2,0,1:T(8,128)(2,1)S(1)}, bf16[8,8,128]{2,0,1:T(8,128)(2,1)S(1)}, u32[]{:S(2)}, u32[]{:S(2)}) collective-permute-start(bf16[8,8,128]{2,0,1:T(8,128)(2,1)S(1)} %get-tuple-element.12), channel_id=1, source_target_pairs={{0,30},{1,31},{2,0},{3,1},{4,2},{5,3},{6,4},{7,5},{8,6},{9,7},{10,... | collective-permute-start | bytes 49160 | tf_op jit(solution)/shard_map/ppermute | solution.py:9
  9.6 23.8 %collective-permute-start.1 = (bf16[8,8,128]{2,0,1:T(8,128)(2,1)S(1)}, bf16[8,8,128]{2,0,1:T(8,128)(2,1)S(1)}, u32[]{:S(2)}, u32[]{:S(2)}) collective-permute-start(bf16[8,8,128]{2,0,1:T(8,128)(2,1)S(1)} %get-tuple-element.11), channel_id=1, source_target_pairs={{0,31},{1,0},{2,1},{3,2},{4,3},{5,4},{6,5},{7,6},{8,7},{9,8},{10,9... | collective-permute-start | bytes 49160 | tf_op jit(solution)/shard_map/ppermute | solution.py:9
  9.6 23.9 %collective-permute-start.2 = (bf16[8,8,128]{2,0,1:T(8,128)(2,1)S(1)}, bf16[8,8,128]{2,0,1:T(8,128)(2,1)S(1)}, u32[]{:S(2)}, u32[]{:S(2)}) collective-permute-start(bf16[8,8,128]{2,0,1:T(8,128)(2,1)S(1)} %get-tuple-element.10), channel_id=1, source_target_pairs={{0,0},{1,1},{2,2},{3,3},{4,4},{5,5},{6,6},{7,7},{8,8},{9,9},{10,10... | collective-permute-start | bytes 49160 | tf_op jit(solution)/shard_map/ppermute | solution.py:9
  9.6 23.9 %collective-permute-start.3 = (bf16[8,8,128]{2,0,1:T(8,128)(2,1)S(1)}, bf16[8,8,128]{2,0,1:T(8,128)(2,1)S(1)}, u32[]{:S(2)}, u32[]{:S(2)}) collective-permute-start(bf16[8,8,128]{2,0,1:T(8,128)(2,1)S(1)} %get-tuple-element.9), channel_id=1, source_target_pairs={{0,1},{1,2},{2,3},{3,4},{4,5},{5,6},{6,7},{7,8},{8,9},{9,10},{10,1... | collective-permute-start | bytes 49160 | tf_op jit(solution)/shard_map/ppermute | solution.py:9
  10.2 23.4 %collective-permute-start.4 = (bf16[8,8,128]{2,0,1:T(8,128)(2,1)S(1)}, bf16[8,8,128]{2,0,1:T(8,128)(2,1)S(1)}, u32[]{:S(2)}, u32[]{:S(2)}) collective-permute-start(bf16[8,8,128]{2,0,1:T(8,128)(2,1)S(1)} %get-tuple-element.8), channel_id=1, source_target_pairs={{0,2},{1,3},{2,4},{3,5},{4,6},{5,7},{6,8},{7,9},{8,10},{9,11},{10,... | collective-permute-start | bytes 49160 | tf_op jit(solution)/shard_map/ppermute | solution.py:9
  22.3 5.8 %copy-start.6 = (s32[1,5,8]{2,0,1:T(1,128)S(1)}, s32[1,5,8]{2,0,1:T(1,128)}, u32[]{:S(2)}) copy-start(s32[1,5,8]{2,0,1:T(1,128)} %param.14) | copy-start | bytes 484
  28.1 5.5 %copy-start.3 = (bf16[1,5,8,128,128]{4,3,2,1,0:T(8,128)(2,1)S(1)}, bf16[1,5,8,128,128]{4,3,2,1,0:T(8,128)(2,1)}, u32[]{:S(2)}) copy-start(bf16[1,5,8,128,128]{4,3,2,1,0:T(8,128)(2,1)} %param.16) | copy-start | bytes 3932164
  28.1 6.4 %copy-start.7 = (f32[2,8]{1,0:T(2,128)S(1)}, f32[2,8]{1,0:T(2,128)}, u32[]{:S(2)}) copy-start(f32[2,8]{1,0:T(2,128)} %param.17) | copy-start | bytes 196
  34.5 7.6 %copy-start.4 = (f32[8,4096]{1,0:T(8,128)}, f32[8,4096]{1,0:T(8,128)S(1)}, u32[]{:S(2)}) copy-start(f32[8,4096]{1,0:T(8,128)S(1)} %bitcast_multiply_fusion.1) | copy-start | bytes 393220
  46.6 2.2 %copy-start.1 = (f32[2,128,4096]{1,2,0:T(8,128)S(1)}, f32[2,128,4096]{1,2,0:T(8,128)}, u32[]{:S(2)}) copy-start(f32[2,128,4096]{1,2,0:T(8,128)} %copy.36) | copy-start | bytes 12582916
  52.8 4.2 %copy-start.9 = (s32[1,4,2,128]{3,2,1,0:T(2,128)S(1)}, s32[1,4,2,128]{3,2,1,0:T(2,128)}, u32[]{:S(2)}) copy-start(s32[1,4,2,128]{3,2,1,0:T(2,128)} %param.21) | copy-start | bytes 12292
  63.0 12.6 %collective-permute-start.5 = (bf16[2,2,128,128]{3,0,2,1:T(2,128)(2,1)S(1)}, bf16[2,2,128,128]{3,0,2,1:T(2,128)(2,1)S(1)}, u32[]{:S(2)}, u32[]{:S(2)}) collective-permute-start(bf16[2,2,128,128]{3,0,2,1:T(2,128)(2,1)S(1)} %get-tuple-element.4), channel_id=1, source_target_pairs={{0,30},{1,31},{2,0},{3,1},{4,2},{5,3},{6,4},{7,5},{8,6},{9,7},{10,... | collective-permute-start | bytes 393224 | tf_op jit(solution)/shard_map/ppermute | solution.py:9
  68.0 7.6 %collective-permute-start.6 = (bf16[2,2,128,128]{3,0,2,1:T(2,128)(2,1)S(1)}, bf16[2,2,128,128]{3,0,2,1:T(2,128)(2,1)S(1)}, u32[]{:S(2)}, u32[]{:S(2)}) collective-permute-start(bf16[2,2,128,128]{3,0,2,1:T(2,128)(2,1)S(1)} %get-tuple-element.7), channel_id=1, source_target_pairs={{0,31},{1,0},{2,1},{3,2},{4,3},{5,4},{6,5},{7,6},{8,7},{9,8},{10,9... | collective-permute-start | bytes 393224 | tf_op jit(solution)/shard_map/ppermute | solution.py:9
  68.7 8.8 %collective-permute-start.7 = (bf16[2,2,128,128]{3,0,2,1:T(2,128)(2,1)S(1)}, bf16[2,2,128,128]{3,0,2,1:T(2,128)(2,1)S(1)}, u32[]{:S(2)}, u32[]{:S(2)}) collective-permute-start(bf16[2,2,128,128]{3,0,2,1:T(2,128)(2,1)S(1)} %get-tuple-element.6), channel_id=1, source_target_pairs={{0,1},{1,2},{2,3},{3,4},{4,5},{5,6},{6,7},{7,8},{8,9},{9,10},{10,1... | collective-permute-start | bytes 393224 | tf_op jit(solution)/shard_map/ppermute | solution.py:9
  68.7 10.0 %collective-permute-start.8 = (bf16[2,2,128,128]{3,0,2,1:T(2,128)(2,1)S(1)}, bf16[2,2,128,128]{3,0,2,1:T(2,128)(2,1)S(1)}, u32[]{:S(2)}, u32[]{:S(2)}) collective-permute-start(bf16[2,2,128,128]{3,0,2,1:T(2,128)(2,1)S(1)} %get-tuple-element.5), channel_id=1, source_target_pairs={{0,2},{1,3},{2,4},{3,5},{4,6},{5,7},{6,8},{7,9},{8,10},{9,11},{10,... | collective-permute-start | bytes 393224 | tf_op jit(solution)/shard_map/ppermute | solution.py:9
  70.0 12.8 %copy-start.10 = (s32[1,4,2,128]{3,2,1,0:T(2,128)S(1)}, s32[1,4,2,128]{3,2,1,0:T(2,128)}, u32[]{:S(2)}) copy-start(s32[1,4,2,128]{3,2,1,0:T(2,128)} %param.22) | copy-start | bytes 12292
  78.7 0.7 copy-start.5
  82.8 20.4 %copy-start.2 = (f32[2,128,4096]{2,1,0:T(8,128)S(1)}, f32[2,128,4096]{2,1,0:T(8,128)}, u32[]{:S(2)}) copy-start(f32[2,128,4096]{2,1,0:T(8,128)} %copy.41) | copy-start | bytes 12582916
where the time goes:
time: 114 us; the launch traced here: 113 us
  matrix products  50.2 us (44%)
  local copies, waits for them, and re-layouts  30.6 us (27%)
  starting transfers between devices  15 us (13%)
  other arithmetic  13.5 us (12%)
  waiting for transfers between devices  3.08 us (3%)
    dot_general x1, matrix products, body(): lax.dot_general(flat_mixed, ghost_table, (((1,), (1,)), ((), ())), precis...  20.4 us
    ppermute x9, starting transfers between devices, shifted(): lax.ppermute(array, axis, [(i, (i + by) % length) for i in range(length)])  15 us
    dot_general x1, matrix products, body(): added = jnp.dot(increment, ghost_table, precision=lax.Precision.HIGHEST)  10.1 us
    unnamed x28, local copies, waits for them, and re-layouts  8.42 us
    dot_general x1, matrix products, body(): ghost_wet = jnp.dot(ghost_table, wetf, precision=lax.Precision.HIGHEST)  8.22 us
    add x1, local copies, waits for them, and re-layouts, body(): mixed = wetf * solved + (1.0 - wetf) * tracer  5.65 us
    slice x1, local copies, waits for them, and re-layouts, body(): tracer[:, 1:, :]  5.38 us
    dot_general x1, matrix products, body(): jnp.dot(sent.reshape(tracers * levels, ocean_cells), source_table, prefer...  4.92 us
  transfers between devices with their start and end apart: 9, of which 2 were waited for; matrix products, arithmetic and copies ran while one was open for 25% of the time, Pallas kernels for 0%

commit v1 on v0

--- a/solution.py
+++ b/solution.py
@@ -72,7 +72,7 @@
     rhs = jnp.concatenate([tracer[:, 0:1, :] + surface[:, None, :], tracer[:, 1:, :]], axis=1)
     shaped = rhs.reshape(tracers, levels, ocean_blocks, block_cells)
     solved = jnp.einsum(
-        "blk,tkbc->tlbc", mix_inverse, shaped, precision=lax.Precision.HIGHEST
+        "blk,tkbc->tlbc", mix_inverse, shaped, precision=lax.Precision.HIGH
     ).reshape(tracers, levels, ocean_cells)
     mixed = wetf * solved + (1.0 - wetf) * tracer
     sent = mixed.astype(jnp.bfloat16)
@@ -96,24 +96,19 @@
     values = (
         jnp.transpose(received, (2, 3, 0, 1, 4))
         .reshape(tracers * levels, picks)
-        .astype(jnp.float32)
     )
-    ghost_table = (halo_ghost[0].reshape(-1)[:, None] == cell_ids[None, :]).astype(jnp.float32)
+    rows_used = jnp.arange(halo_depth, dtype=jnp.int32)[None, :] < halo_rows[0][:, None]
+    used = jnp.broadcast_to(rows_used[:, :, None], (halo_count, halo_depth, lanes)).reshape(-1)
+    ghost_table = (
+        (halo_ghost[0].reshape(-1)[:, None] == cell_ids[None, :]) & used[:, None]
+    ).astype(jnp.bfloat16)
     flat_mixed = mixed.reshape(tracers * levels, ocean_cells)
-    current = lax.dot_general(
-        flat_mixed, ghost_table, (((1,), (1,)), ((), ())), precision=lax.Precision.HIGHEST
+    summed = jnp.dot(values, ghost_table, preferred_element_type=jnp.float32)
+    hits = jnp.sum(ghost_table.astype(jnp.float32), axis=0)
+    pull = 0.25 * wetf
+    tracer_out = (flat_mixed + pull[None, :] * (summed - hits[None, :] * flat_mixed)).reshape(
+        tracers, levels, ocean_cells
     )
-    ghost_wet = jnp.dot(ghost_table, wetf, precision=lax.Precision.HIGHEST)
-    rows_used = (jnp.arange(halo_depth, dtype=jnp.int32)[None, :] < halo_rows[0][:, None]).astype(
-        jnp.float32
-    )
-    weight = (
-        jnp.broadcast_to(rows_used[:, :, None], (halo_count, halo_depth, lanes)).reshape(-1)
-        * ghost_wet
-    )
-    increment = 0.25 * (values - current) * weight[None, :]
-    added = jnp.dot(increment, ghost_table, precision=lax.Precision.HIGHEST)
-    tracer_out = (flat_mixed + added).reshape(tracers, levels, ocean_cells)
     return (ocean_flux, tracer_out)
 
 

time: 114 us -> 86.8 us (0.76)
  matrix products: 50.2 us -> 19.4 us
  other arithmetic: 13.5 us -> 22.2 us
  waiting for transfers between devices: 3.08 us -> 0.02 us
  local copies, waits for them, and re-layouts: 30.6 us -> 28.5 us
    dot_general x3 -> x1, matrix products: 38.7 us -> 10.3 us  [body(): summed = jnp.dot(values, ghost_table, preferred_element_type=jnp.float32)]
    mul x1 -> x2, other arithmetic: 0.01 us -> 5.54 us  [the longest x1 4.82 us: body(): hits[None, :] * flat_mixed]
    reduce_sum x0 -> x1, other arithmetic: none -> 4.06 us  [body(): hits = jnp.sum(ghost_table.astype(jnp.float32), axis=0)]
    ppermute x9, waiting for transfers between devices: 3.08 us -> 0.02 us  [shifted(): lax.ppermute(array, axis, [(i, (i + by) % length) for i in range(length)])]
    dot_general x1, matrix products: 4.47 us -> 2.16 us  [body(): jnp.einsum('blk,tkbc->tlbc', mix_inverse, shaped, precision=lax.Precision...]
    convert_element_type x1 -> x0, local copies, waits for them, and re-layouts: 1.81 us -> none  [body(): values = jnp.transpose(received, (2, 3, 0, 1, 4)).reshape(tracers * level...]
    convert_element_type x2 -> x0, other arithmetic: 1.69 us -> none  [the longest x1 1.62 us: body(): values = jnp.transpose(received, (2, 3, 0, 1, 4)).reshape(tracers * level...]
    unnamed x28 -> x22, local copies, waits for them, and re-layouts: 8.42 us -> 7.75 us
  transfers between devices with their start and end apart: 9 -> 9, of which waited for: 2 -> 0; matrix products, arithmetic and copies ran while one was open for 25% -> 34% of each run, Pallas kernels for 0% -> 0%
where the time goes in v1:
time: 86.8 us; the launch traced here: 86.1 us
  local copies, waits for them, and re-layouts  28.5 us (33%)
  other arithmetic  22.2 us (26%)
  matrix products  19.4 us (22%)
  starting transfers between devices  15.1 us (17%)
  between operations  0.88 us (1%)
    ppermute x9, starting transfers between devices, shifted(): lax.ppermute(array, axis, [(i, (i + by) % length) for i in range(length)])  15.1 us
    dot_general x1, matrix products, body(): summed = jnp.dot(values, ghost_table, preferred_element_type=jnp.float32)  10.3 us
    unnamed x22, local copies, waits for them, and re-layouts  7.75 us
    add x1, local copies, waits for them, and re-layouts, body(): mixed = wetf * solved + (1.0 - wetf) * tracer  5.61 us
    slice x1, local copies, waits for them, and re-layouts, body(): tracer[:, 1:, :]  5.39 us
    dot_general x1, matrix products, body(): jnp.dot(sent.reshape(tracers * levels, ocean_cells), source_table, prefer...  4.91 us
    mul x1, other arithmetic, body(): hits[None, :] * flat_mixed  4.82 us
    concatenate x1, other arithmetic, body(): jnp.concatenate([tracer[:, 0:1, :] + surface[:, None, :], tracer[:, 1:, :...  4.61 us
  transfers between devices with their start and end apart: 9, of which 0 were waited for; matrix products, arithmetic and copies ran while one was open for 34% of the time, Pallas kernels for 0%

profile of v1, /device:TPU:0, one launch (start us, length us, event | category | flops | bytes accessed | tf_op | source)
XLA Modules:
  0.0 86.1 jit_solution(11049014576783922513)
XLA Ops:
  0.6 0.8 reduce
  1.6 1.0 %convolution_convert_fusion = bf16[40,8,128]{2,0,1:T(8,128)(2,1)S(1)} fusion(bf16[8,24,128]{2,0,1:T(8,128)(2,1)} %bitcast.95, s32[40]{0:T(128)S(1)} %eq.60), kind=kOutput, calls=%fused_computation.28 | convolution fusion | flops 2008000 | bytes 131232 | tf_op jit(solution)/shard_map/sa,fab->sfb/dot_general | solution.py:49
  2.6 7.0 %collective-permute-start = (bf16[8,8,128]{2,0,1:T(8,128)(2,1)S(1)}, bf16[8,8,128]{2,0,1:T(8,128)(2,1)S(1)}, u32[]{:S(2)}, u32[]{:S(2)}) collective-permute-start(bf16[8,8,128]{2,0,1:T(8,128)(2,1)S(1)} %get-tuple-element.12), channel_id=1, source_target_pairs={{0,30},{1,31},{2,0},{3,1},{4,2},{5,3},{6,4},{7,5},{8,6},{9,7},{10,... | collective-permute-start | bytes 49160 | tf_op jit(solution)/shard_map/ppermute | solution.py:9
  9.6 0.5 collective-permute-start.3
  10.1 0.7 collective-permute-start.4
  10.8 0.7 broadcast_multiply_fusion
  11.5 0.7 iota_compare_fusion.8
  12.4 4.1 %convert_reduce_fusion = f32[4096]{0:T(1024)S(1)} fusion(s32[1024]{0:T(1024)} %bitcast.99, pred[1024]{0:T(1024)(128)(4,1)S(1)} %and.10), kind=kLoop, calls=%fused_computation | loop fusion | flops 20967424 | bytes 21504 | tf_op jit(solution)/shard_map/reduce_sum | solution.py:107
  16.4 0.7 fusion.40
  17.1 0.7 convert_element_type.30
  17.9 1.0 %slice.43 = f32[2,1,4096]{2,1,0:T(1,128)S(1)} slice(f32[2,128,4096]{2,1,0:T(8,128)} %param.18), slice={[0:2], [0:1], [0:4096]} | slice | bytes 65536 | tf_op jit(solution)/shard_map/slice | solution.py:72
  18.9 5.8 %copy.51 = f32[2,128,4096]{1,2,0:T(8,128)} copy(f32[2,128,4096]{2,1,0:T(8,128)} %param.18) | data formatting | bytes 8388608 | tf_op args[6]
  24.7 5.4 %slice.54 = f32[2,127,4096]{1,2,0:T(8,128)} slice(f32[2,128,4096]{1,2,0:T(8,128)} %copy.51), slice={[0:2], [1:128], [0:4096]} | slice | bytes 8323072 | tf_op jit(solution)/shard_map/slice | solution.py:72
  30.2 0.4 fusion.28
  31.3 2.7 %copy.52 = f32[2,1,4096]{1,2,0:T(8,128)} copy(f32[2,1,4096]{2,0,1:T(2,128)S(1)} %fusion.17) | data formatting | bytes 65536 | tf_op jit(solution)/shard_map/add | solution.py:72
  34.0 4.6 %pad_maximum_fusion = f32[2,128,4096]{1,2,0:T(8,128)S(1)} fusion(f32[2,127,4096]{1,2,0:T(8,128)} %slice.54, f32[2,1,4096]{1,2,0:T(8,128)} %copy.52), kind=kLoop, calls=%fused_computation.15 | loop fusion | flops 1048576 | bytes 8388608 | tf_op jit(solution)/shard_map/concatenate | solution.py:72
  38.7 2.2 %fusion.21 = f32[2,128,32,128]{1,3,0,2:T(8,128)S(1)} fusion(f32[2,128,32,128]{1,3,2,0:T(8,128)S(1)} %bitcast.87, f32[32,128,128]{2,1,0:T(8,128)S(1)} %copy-done), kind=kOutput, calls=%fused_computation.21 | convolution fusion | flops 805306368 | bytes 10485760 | tf_op jit(solution)/shard_map/blk,tkbc->tlbc/dot_general | solution.py:74
  41.1 1.9 %copy-done.1 = f32[2,128,4096]{1,2,0:T(8,128)S(1)} copy-done((f32[2,128,4096]{1,2,0:T(8,128)S(1)}, f32[2,128,4096]{1,2,0:T(8,128)}, u32[]{:S(2)}) %copy-start.1) | copy-done | bytes 4194328
  43.0 4.1 %fusion.41 = (bf16[2,128,4096]{1,2,0:T(8,128)(2,1)}, f32[2,128,4096]{1,2,0:T(8,128)}) fusion(f32[2,128,4096]{1,2,0:T(8,128)S(1)} %copy-done.1, f32[4096]{0:T(1024)S(1)} %get-tuple-element.14, f32[2,128,32,128]{1,3,2,0:T(8,128)S(1)} %copy.54, f32[4096]{0:T(1024)S(1)} %convert_element_type.30), kind=kLoop, calls=%fused_computation.56 | loop fusion | flops 4194304 | bytes 14712832 | tf_op jit(solution)/shard_map/convert_element_type | solution.py:78
  47.1 4.1 %copy.57 = bf16[2,128,4096]{2,1,0:T(8,128)(2,1)} copy(bf16[2,128,4096]{1,2,0:T(8,128)(2,1)} %get-tuple-element.2) | data formatting | bytes 4194304 | tf_op jit(solution)/shard_map/convert_element_type | solution.py:78
  51.2 4.9 %fusion.27 = bf16[256,1024]{1,0:T(8,128)(2,1)S(1)} fusion(bf16[256,4096]{1,0:T(8,128)(2,1)} %bitcast.89, s32[1024]{0:T(1024)S(1)} %bitcast.98), kind=kOutput, calls=%fused_computation.25 | convolution fusion | flops 2151940096 | bytes 2625536 | tf_op jit(solution)/shard_map/dot_general | solution.py:85
  56.1 0.4 reshape.107
  56.5 0.4 copy.81
  56.9 0.4 slice_bitcast_fusion.3
  57.2 5.0 %collective-permute-start.5 = (bf16[2,2,128,128]{3,0,2,1:T(2,128)(2,1)S(1)}, bf16[2,2,128,128]{3,0,2,1:T(2,128)(2,1)S(1)}, u32[]{:S(2)}, u32[]{:S(2)}) collective-permute-start(bf16[2,2,128,128]{3,0,2,1:T(2,128)(2,1)S(1)} %get-tuple-element.4), channel_id=1, source_target_pairs={{0,30},{1,31},{2,0},{3,1},{4,2},{5,3},{6,4},{7,5},{8,6},{9,7},{10,... | collective-permute-start | bytes 393224 | tf_op jit(solution)/shard_map/ppermute | solution.py:9
  62.3 0.7 collective-permute-start.6
  62.9 1.2 %collective-permute-start.8 = (bf16[2,2,128,128]{3,0,2,1:T(2,128)(2,1)S(1)}, bf16[2,2,128,128]{3,0,2,1:T(2,128)(2,1)S(1)}, u32[]{:S(2)}, u32[]{:S(2)}) collective-permute-start(bf16[2,2,128,128]{3,0,2,1:T(2,128)(2,1)S(1)} %get-tuple-element.5), channel_id=1, source_target_pairs={{0,2},{1,3},{2,4},{3,5},{4,6},{5,7},{6,8},{7,9},{8,10},{9,11},{10,... | collective-permute-start | bytes 393224 | tf_op jit(solution)/shard_map/ppermute | solution.py:9
  64.1 5.6 %copy.56 = f32[2,128,4096]{2,1,0:T(8,128)} copy(f32[2,128,4096]{1,2,0:T(8,128)} %get-tuple-element.3) | data formatting | bytes 8388608 | tf_op jit(solution)/shard_map/add | solution.py:77
  69.7 4.8 %bitcast_multiply_fusion = f32[256,4096]{1,0:T(8,128)} fusion(f32[2,128,4096]{2,1,0:T(8,128)} %copy.56, f32[4096]{0:T(1024)S(1)} %convert_reduce_fusion), kind=kLoop, calls=%fused_computation.16 | loop fusion | flops 1048576 | bytes 8404992 | tf_op jit(solution)/shard_map/mul | solution.py:109
  74.6 0.8 maximum_bitcast_fusion
  75.4 0.4 reshape.108
  75.8 10.3 %fusion.14 = f32[256,4096]{1,0:T(8,128)} fusion(f32[256,4096]{1,0:T(8,128)} %bitcast.88, f32[256,4096]{1,0:T(8,128)} %bitcast_multiply_fusion, bf16[256,1024]{1,0:T(8,128)(2,1)S(1)} %reshape.108, s32[1024]{0:T(1024)S(1)} %bitcast.100, pred[1024]{0:T(1024)(128)(4,1)S(1)} %and.10, f32[4096]{0:T(1024)S(1)} %get-tuple-element.13), kind=kOutput, calls=%fused_computation.12 | convolution fusion | flops 2159017984 | bytes 13128704 | tf_op jit(solution)/shard_map/dot_general | solution.py:106
  (41 shorter events, 1.2 us)
Async XLA Ops:
  0.6 38.0 %copy-start = (f32[32,128,128]{2,1,0:T(8,128)S(1)}, f32[32,128,128]{2,1,0:T(8,128)}, u32[]{:S(2)}) copy-start(f32[32,128,128]{2,1,0:T(8,128)} %param.20) | copy-start | bytes 6291460
  2.6 27.4 %collective-permute-start = (bf16[8,8,128]{2,0,1:T(8,128)(2,1)S(1)}, bf16[8,8,128]{2,0,1:T(8,128)(2,1)S(1)}, u32[]{:S(2)}, u32[]{:S(2)}) collective-permute-start(bf16[8,8,128]{2,0,1:T(8,128)(2,1)S(1)} %get-tuple-element.12), channel_id=1, source_target_pairs={{0,30},{1,31},{2,0},{3,1},{4,2},{5,3},{6,4},{7,5},{8,6},{9,7},{10,... | collective-permute-start | bytes 49160 | tf_op jit(solution)/shard_map/ppermute | solution.py:9
  9.6 20.4 %collective-permute-start.1 = (bf16[8,8,128]{2,0,1:T(8,128)(2,1)S(1)}, bf16[8,8,128]{2,0,1:T(8,128)(2,1)S(1)}, u32[]{:S(2)}, u32[]{:S(2)}) collective-permute-start(bf16[8,8,128]{2,0,1:T(8,128)(2,1)S(1)} %get-tuple-element.11), channel_id=1, source_target_pairs={{0,31},{1,0},{2,1},{3,2},{4,3},{5,4},{6,5},{7,6},{8,7},{9,8},{10,9... | collective-permute-start | bytes 49160 | tf_op jit(solution)/shard_map/ppermute | solution.py:9
  9.6 20.4 %collective-permute-start.2 = (bf16[8,8,128]{2,0,1:T(8,128)(2,1)S(1)}, bf16[8,8,128]{2,0,1:T(8,128)(2,1)S(1)}, u32[]{:S(2)}, u32[]{:S(2)}) collective-permute-start(bf16[8,8,128]{2,0,1:T(8,128)(2,1)S(1)} %get-tuple-element.10), channel_id=1, source_target_pairs={{0,0},{1,1},{2,2},{3,3},{4,4},{5,5},{6,6},{7,7},{8,8},{9,9},{10,10... | collective-permute-start | bytes 49160 | tf_op jit(solution)/shard_map/ppermute | solution.py:9
  9.6 20.5 %collective-permute-start.3 = (bf16[8,8,128]{2,0,1:T(8,128)(2,1)S(1)}, bf16[8,8,128]{2,0,1:T(8,128)(2,1)S(1)}, u32[]{:S(2)}, u32[]{:S(2)}) collective-permute-start(bf16[8,8,128]{2,0,1:T(8,128)(2,1)S(1)} %get-tuple-element.9), channel_id=1, source_target_pairs={{0,1},{1,2},{2,3},{3,4},{4,5},{5,6},{6,7},{7,8},{8,9},{9,10},{10,1... | collective-permute-start | bytes 49160 | tf_op jit(solution)/shard_map/ppermute | solution.py:9
  10.1 20.0 %collective-permute-start.4 = (bf16[8,8,128]{2,0,1:T(8,128)(2,1)S(1)}, bf16[8,8,128]{2,0,1:T(8,128)(2,1)S(1)}, u32[]{:S(2)}, u32[]{:S(2)}) collective-permute-start(bf16[8,8,128]{2,0,1:T(8,128)(2,1)S(1)} %get-tuple-element.8), channel_id=1, source_target_pairs={{0,2},{1,3},{2,4},{3,5},{4,6},{5,7},{6,8},{7,9},{8,10},{9,11},{10,... | collective-permute-start | bytes 49160 | tf_op jit(solution)/shard_map/ppermute | solution.py:9
  18.8 5.8 %copy-start.4 = (s32[1,5,8]{2,0,1:T(1,128)S(1)}, s32[1,5,8]{2,0,1:T(1,128)}, u32[]{:S(2)}) copy-start(s32[1,5,8]{2,0,1:T(1,128)} %param.14) | copy-start | bytes 484
  24.6 5.5 %copy-start.2 = (bf16[1,5,8,128,128]{4,3,2,1,0:T(8,128)(2,1)S(1)}, bf16[1,5,8,128,128]{4,3,2,1,0:T(8,128)(2,1)}, u32[]{:S(2)}) copy-start(bf16[1,5,8,128,128]{4,3,2,1,0:T(8,128)(2,1)} %param.16) | copy-start | bytes 3932164
  24.6 6.4 %copy-start.5 = (f32[2,8]{1,0:T(2,128)S(1)}, f32[2,8]{1,0:T(2,128)}, u32[]{:S(2)}) copy-start(f32[2,8]{1,0:T(2,128)} %param.17) | copy-start | bytes 196
  31.0 7.6 %copy-start.3 = (f32[8,4096]{1,0:T(8,128)}, f32[8,4096]{1,0:T(8,128)S(1)}, u32[]{:S(2)}) copy-start(f32[8,4096]{1,0:T(8,128)S(1)} %bitcast_multiply_fusion.2) | copy-start | bytes 393220
  40.8 2.2 %copy-start.1 = (f32[2,128,4096]{1,2,0:T(8,128)S(1)}, f32[2,128,4096]{1,2,0:T(8,128)}, u32[]{:S(2)}) copy-start(f32[2,128,4096]{1,2,0:T(8,128)} %copy.51) | copy-start | bytes 12582916
  47.1 4.1 %copy-start.6 = (s32[1,4,2,128]{3,2,1,0:T(2,128)S(1)}, s32[1,4,2,128]{3,2,1,0:T(2,128)}, u32[]{:S(2)}) copy-start(s32[1,4,2,128]{3,2,1,0:T(2,128)} %param.21) | copy-start | bytes 12292
  57.2 17.3 %collective-permute-start.5 = (bf16[2,2,128,128]{3,0,2,1:T(2,128)(2,1)S(1)}, bf16[2,2,128,128]{3,0,2,1:T(2,128)(2,1)S(1)}, u32[]{:S(2)}, u32[]{:S(2)}) collective-permute-start(bf16[2,2,128,128]{3,0,2,1:T(2,128)(2,1)S(1)} %get-tuple-element.4), channel_id=1, source_target_pairs={{0,30},{1,31},{2,0},{3,1},{4,2},{5,3},{6,4},{7,5},{8,6},{9,7},{10,... | collective-permute-start | bytes 393224 | tf_op jit(solution)/shard_map/ppermute | solution.py:9
  62.3 12.3 %collective-permute-start.6 = (bf16[2,2,128,128]{3,0,2,1:T(2,128)(2,1)S(1)}, bf16[2,2,128,128]{3,0,2,1:T(2,128)(2,1)S(1)}, u32[]{:S(2)}, u32[]{:S(2)}) collective-permute-start(bf16[2,2,128,128]{3,0,2,1:T(2,128)(2,1)S(1)} %get-tuple-element.7), channel_id=1, source_target_pairs={{0,31},{1,0},{2,1},{3,2},{4,3},{5,4},{6,5},{7,6},{8,7},{9,8},{10,9... | collective-permute-start | bytes 393224 | tf_op jit(solution)/shard_map/ppermute | solution.py:9
  62.9 11.6 %collective-permute-start.7 = (bf16[2,2,128,128]{3,0,2,1:T(2,128)(2,1)S(1)}, bf16[2,2,128,128]{3,0,2,1:T(2,128)(2,1)S(1)}, u32[]{:S(2)}, u32[]{:S(2)}) collective-permute-start(bf16[2,2,128,128]{3,0,2,1:T(2,128)(2,1)S(1)} %get-tuple-element.6), channel_id=1, source_target_pairs={{0,1},{1,2},{2,3},{3,4},{4,5},{5,6},{6,7},{7,8},{8,9},{9,10},{10,1... | collective-permute-start | bytes 393224 | tf_op jit(solution)/shard_map/ppermute | solution.py:9
  62.9 11.6 %collective-permute-start.8 = (bf16[2,2,128,128]{3,0,2,1:T(2,128)(2,1)S(1)}, bf16[2,2,128,128]{3,0,2,1:T(2,128)(2,1)S(1)}, u32[]{:S(2)}, u32[]{:S(2)}) collective-permute-start(bf16[2,2,128,128]{3,0,2,1:T(2,128)(2,1)S(1)} %get-tuple-element.5), channel_id=1, source_target_pairs={{0,2},{1,3},{2,4},{3,5},{4,6},{5,7},{6,8},{7,9},{8,10},{9,11},{10,... | collective-permute-start | bytes 393224 | tf_op jit(solution)/shard_map/ppermute | solution.py:9
  69.7 6.1 %copy-start.7 = (s32[1,4,2,128]{3,2,1,0:T(2,128)S(1)}, s32[1,4,2,128]{3,2,1,0:T(2,128)}, u32[]{:S(2)}) copy-start(s32[1,4,2,128]{3,2,1,0:T(2,128)} %param.22) | copy-start | bytes 12292

commit v2 on v1

v2 whole, which is shorter than its diff:
```python
import jax
import jax.numpy as jnp
from jax import lax
from jax.experimental import pallas as pl
from jax.experimental.pallas import tpu as pltpu
from jax.sharding import PartitionSpec as P

MESH = pl.DeviceIdType.MESH
CHUNKS = 8
TILE = 1024


def split(value):
    high = value.astype(jnp.bfloat16)
    return high, (value - high.astype(jnp.float32)).astype(jnp.bfloat16)


def product(left, right):
    return jnp.dot(left, right, preferred_element_type=jnp.float32)


def couple_kernel(
    remap_send,
    remap_target,
    remap_counts,
    coupling,
    atm,
    wet,
    halo_send,
    weights_hbm,
    tracer_hbm,
    inverse_hbm,
    flux_out,
    mixed,
    received,
    weights,
    tracer,
    inverse,
    sent,
    surface,
    total,
    outgoing,
    arrived,
    tables,
    picked,
    load_sem,
    flux_send_sem,
    flux_recv_sem,
    halo_send_sem,
    halo_recv_sem,
):
    size = lax.axis_size("patch")
    me = lax.axis_index("patch")
    spans, slots = remap_send.shape[1], remap_send.shape[2]
    radius = spans // 2
    tracers, levels, cells = tracer.shape
    block = weights.shape[-1]
    blocks = cells // block
    fluxes = atm.shape[0]
    steps = [d - radius for d in range(spans) if d != radius]
    depth, lanes = halo_send.shape[2], halo_send.shape[3]

    def peer(step):
        return lax.rem(me + step + size, size)

    weight_load = pltpu.make_async_copy(weights_hbm.at[0], weights, load_sem.at[2 * CHUNKS])
    weight_load.start()
    part, span = blocks // CHUNKS, cells // CHUNKS
    loads = []
    for chunk in range(CHUNKS):
        run = pl.ds(chunk * span, span)
        loads.append(
            pltpu.make_async_copy(
                tracer_hbm.at[:, :, run], tracer.at[:, :, run], load_sem.at[2 * chunk]
            )
        )
        group = pl.ds(chunk * part, part)
        loads.append(
            pltpu.make_async_copy(
                inverse_hbm.at[group], inverse.at[group], load_sem.at[2 * chunk + 1]
            )
        )
    for load in loads:
        load.start()

    barrier = pltpu.get_barrier_semaphore()
    for step in steps:
        pl.semaphore_signal(barrier, inc=1, device_id=(peer(step),), device_id_type=MESH)
    sources = [
        atm[:, a * block : (a + 1) * block].astype(jnp.float32)
        for a in range(atm.shape[1] // block)
    ]
    blank = jnp.zeros((fluxes, block), jnp.int32)
    for d in range(spans):
        for c in range(slots):
            wanted = blank + remap_send[0, d, c]
            piece = sources[0]
            for a in range(1, len(sources)):
                piece = jnp.where(wanted == a, sources[a], piece)
            piece = piece.astype(jnp.bfloat16)
            if d == radius:
                arrived[d, c] = piece
            else:
                outgoing[d, c] = piece
    pl.semaphore_wait(barrier, len(steps))
    flux_copies = []
    for d in range(spans):
        if d == radius:
            continue
        copy = pltpu.make_async_remote_copy(
            src_ref=outgoing.at[d],
            dst_ref=arrived.at[d],
            send_sem=flux_send_sem.at[d],
            recv_sem=flux_recv_sem.at[d],
            device_id=(peer(d - radius),),
            device_id_type=MESH,
        )
        copy.start()
        flux_copies.append(copy)

    rows = 512

    def table_rows(index, _):
        base = pl.multiple_of(index * rows, rows)
        ids = lax.broadcasted_iota(jnp.int32, (rows, lanes), 0) + base
        for h in range(len(steps)):
            for r in range(depth):
                hit = ids == halo_send[0, h, r : r + 1, :]
                tables[h, pl.ds(base, rows), r * lanes : (r + 1) * lanes] = jnp.where(
                    hit, 1.0, 0.0
                ).astype(jnp.bfloat16)
        return 0

    lax.fori_loop(0, cells // rows, table_rows, 0)

    weight_load.wait()
    for copy in flux_copies:
        copy.wait()
    owner = lax.broadcasted_iota(jnp.int32, (blocks, fluxes, block), 0)
    for d in range(spans):
        pieces = []
        for c in range(slots):
            used = (blank + remap_counts[0, d]) > c
            piece = jnp.where(used, arrived[d, c].astype(jnp.float32), 0.0)
            placed = jnp.where(owner == remap_target[0, d, c], piece[None], 0.0)
            pieces.append(placed.reshape(blocks * fluxes, block).astype(jnp.bfloat16))
        left = jnp.concatenate(pieces, axis=1)
        term = product(left, weights[d].reshape(slots * block, block))
        if d == 0:
            total[...] = term
        else:
            total[...] += term
    for b in range(blocks):
        run = slice(b * block, (b + 1) * block)
        flux = total[b * fluxes : (b + 1) * fluxes, :] * wet[0:1, run].astype(jnp.float32)
        flux_out[:, run] = flux
        for t in range(tracers):
            value = coupling[t, 0] * flux[0:1, :]
            for f in range(1, fluxes):
                value = value + coupling[t, f] * flux[f : f + 1, :]
            surface[t : t + 1, run] = value

    top = lax.broadcasted_iota(jnp.int32, (levels, block), 0) == 0

    def mix_block(k, _):
        run = pl.ds(pl.multiple_of(k * block, block), block)
        high, low = split(inverse[k])
        wetf = wet[0:1, run].astype(jnp.float32)
        held = [tracer[t, :, run] for t in range(tracers)]
        right = jnp.concatenate(
            [
                held[t] + jnp.where(top, surface[t : t + 1, run], 0.0)
                for t in range(tracers)
            ],
            axis=1,
        )
        right_high, right_low = split(right)
        solved = (
            product(high, right_high) + product(high, right_low) + product(low, right_high)
        )
        for t in range(tracers):
            value = wetf * solved[:, t * block : (t + 1) * block] + (1.0 - wetf) * held[t]
            mixed[t, :, run] = value
            sent[t * levels : (t + 1) * levels, run] = value.astype(jnp.bfloat16)
        return 0

    for chunk in range(CHUNKS):
        loads[2 * chunk].wait()
        loads[2 * chunk + 1].wait()
        lax.fori_loop(chunk * part, (chunk + 1) * part, mix_block, 0)

    order = sorted(range(len(steps)), key=lambda h: (-abs(steps[h]), h))
    halo_copies = []
    for h in order:
        picked[h] = product(sent[...], tables[h]).astype(jnp.bfloat16)
        copy = pltpu.make_async_remote_copy(
            src_ref=picked.at[h],
            dst_ref=received.at[h],
            send_sem=halo_send_sem.at[h],
            recv_sem=halo_recv_sem.at[h],
            device_id=(peer(steps[h]),),
            device_id_type=MESH,
        )
        copy.start()
        halo_copies.append(copy)
    for copy in halo_copies:
        copy.wait()


def halo_kernel(halo_rows, halo_ghost, wet, received, flux_in, mixed, flux_out, out):
    tracers, levels, tile = out.shape
    run = pl.ds(pl.multiple_of(pl.program_id(0) * tile, tile), tile)
    hosts, depth, lanes = halo_ghost.shape[1:]
    ids = lax.broadcasted_iota(jnp.int32, (tile, lanes), 0) + pl.program_id(0) * tile
    columns = []
    for h in range(hosts):
        for r in range(depth):
            ghost = jnp.where(r < halo_rows[0, h], halo_ghost[0, h, r : r + 1, :], -1)
            columns.append(jnp.where(ids == ghost, 1.0, 0.0).astype(jnp.bfloat16))
    table = jnp.concatenate(columns, axis=1)
    values = jnp.concatenate([received[h] for h in range(hosts)], axis=1)
    contract = (((1,), (1,)), ((), ()))
    summed = lax.dot_general(values, table, contract, preferred_element_type=jnp.float32)
    ones = jnp.ones((16, table.shape[1]), jnp.bfloat16)
    hits = lax.dot_general(ones, table, contract, preferred_element_type=jnp.float32)[0:1]
    pull = 0.25 * wet[...].astype(jnp.float32)
    for t in range(tracers):
        value = mixed[t, :, run]
        out[t] = value + pull * (summed[t * levels : (t + 1) * levels] - hits * value)
    flux_out[...] = flux_in[...]


def body(
    atm_flux,
    remap_send,
    remap_target,
    remap_counts,
    remap_weights,
    coupling,
    tracer,
    wet,
    mix_inverse,
    halo_send,
    halo_ghost,
    halo_rows,
):
    spans, slots = remap_send.shape[1:]
    block = remap_weights.shape[-1]
    fluxes = atm_flux.shape[0]
    tracers, levels, cells = tracer.shape
    blocks = cells // block
    hosts, depth, lanes = halo_send.shape[1:]
    picks = depth * lanes
    features = tracers * levels
    wet_row = wet.reshape(1, cells)
    vmem = pl.BlockSpec(memory_space=pltpu.VMEM)
    smem = pl.BlockSpec(memory_space=pltpu.SMEM)
    hbm = pl.BlockSpec(memory_space=pltpu.HBM)
    flux, mixed, received = pl.pallas_call(
        couple_kernel,
        out_shape=(
            pltpu.VMEM((fluxes, cells), jnp.float32),
            pltpu.VMEM((tracers, levels, cells), jnp.float32),
            pltpu.VMEM((hosts, features, picks), jnp.bfloat16),
        ),
        in_specs=[smem] * 4 + [vmem] * 3 + [hbm] * 3,
        out_specs=(vmem, vmem, vmem),
        scratch_shapes=[
            pltpu.VMEM((spans, slots, block, block), jnp.bfloat16),
            pltpu.VMEM((tracers, levels, cells), jnp.float32),
            pltpu.VMEM((blocks, levels, levels), jnp.float32),
            pltpu.VMEM((features, cells), jnp.bfloat16),
            pltpu.VMEM((tracers, cells), jnp.float32),
            pltpu.VMEM((blocks * fluxes, block), jnp.float32),
            pltpu.VMEM((spans, slots, fluxes, block), jnp.bfloat16),
            pltpu.VMEM((spans, slots, fluxes, block), jnp.bfloat16),
            pltpu.VMEM((hosts, cells, picks), jnp.bfloat16),
            pltpu.VMEM((hosts, features, picks), jnp.bfloat16),
            pltpu.SemaphoreType.DMA((2 * CHUNKS + 1,)),
            pltpu.SemaphoreType.DMA((spans,)),
            pltpu.SemaphoreType.DMA((spans,)),
            pltpu.SemaphoreType.DMA((hosts,)),
            pltpu.SemaphoreType.DMA((hosts,)),
        ],
        compiler_params=pltpu.CompilerParams(
            collective_id=0, has_side_effects=True, vmem_limit_bytes=58 * 1024 * 1024
        ),
        name="couple",
    )(
        remap_send,
        remap_target,
        remap_counts,
        coupling,
        atm_flux,
        wet_row,
        halo_send,
        remap_weights,
        tracer,
        mix_inverse,
    )
    tile = min(TILE, cells)
    return pl.pallas_call(
        halo_kernel,
        grid=(cells // tile,),
        out_shape=(
            jax.ShapeDtypeStruct((fluxes, cells), jnp.float32),
            jax.ShapeDtypeStruct((tracers, levels, cells), jnp.float32),
        ),
        in_specs=[
            smem,
            pl.BlockSpec(memory_space=pltpu.VMEM),
            pl.BlockSpec((1, tile), lambda i: (0, i)),
            pl.BlockSpec(memory_space=pltpu.VMEM),
            pl.BlockSpec((fluxes, tile), lambda i: (0, i)),
            pl.BlockSpec(memory_space=pltpu.VMEM),
        ],
        out_specs=(
            pl.BlockSpec((fluxes, tile), lambda i: (0, i)),
            pl.BlockSpec((tracers, levels, tile), lambda i: (0, 0, i)),
        ),
        compiler_params=pltpu.CompilerParams(vmem_limit_bytes=32 * 1024 * 1024),
        name="halo",
    )(halo_rows, halo_ghost, wet_row, received, flux, mixed)


def solution(mesh):
    return jax.shard_map(
        body,
        mesh=mesh,
        in_specs=(
            P(None, "patch"),
            P("patch", None, None),
            P("patch", None, None),
            P("patch", None),
            P("patch", None, None, None, None),
            P(),
            P(None, None, "patch"),
            P("patch"),
            P("patch", None, None),
            P("patch", None, None, None),
            P("patch", None, None, None),
            P("patch", None),
        ),
        out_specs=(P(None, "patch"), P(None, None, "patch")),
        check_vma=False,
    )
```

time: 86.8 us -> 42 us (0.48)
  Pallas kernels: 0 us -> 38.4 us
  local copies, waits for them, and re-layouts: 28.5 us -> 2.58 us
  other arithmetic: 22.2 us -> 0 us
  matrix products: 19.4 us -> 0 us
  starting transfers between devices: 15.1 us -> 0 us
    pallas_call x0 -> x2, Pallas kernels: none -> 38.4 us  [the longest x1 31 us: body(): pl.pallas_call(couple_kernel, out_shape=(pltpu.VMEM((fluxes, cells), jnp....]
    dot_general x7 -> x0, matrix products: 19.4 us -> none  [the longest x1 10.3 us: body(): summed = jnp.dot(values, ghost_table, preferred_element_type=jnp.float32)]
    ppermute x9 -> x0, starting transfers between devices: 15.1 us -> none  [shifted(): lax.ppermute(array, axis, [(i, (i + by) % length) for i in range(length)])]
    add x2 -> x0, local copies, waits for them, and re-layouts: 8.32 us -> none  [the longest x1 5.61 us: body(): mixed = wetf * solved + (1.0 - wetf) * tracer]
    slice x3 -> x0, local copies, waits for them, and re-layouts: 6.37 us -> none  [the longest x1 5.39 us: body(): tracer[:, 1:, :]]
    mul x3 -> x0, other arithmetic: 5.62 us -> none  [the longest x1 4.82 us: body(): hits[None, :] * flat_mixed]
    convert_element_type x3 -> x0, other arithmetic: 5.54 us -> none  [the longest x1 4.09 us: body(): sent = mixed.astype(jnp.bfloat16)]
    unnamed x22 -> x8, local copies, waits for them, and re-layouts: 7.75 us -> 2.58 us
  transfers between devices with their start and end apart: 9 -> 0, of which waited for: 0 -> 0; matrix products, arithmetic and copies ran while one was open for 34% -> 0% of each run, Pallas kernels for 0% -> 0%
where the time goes in v2:
time: 42 us; the launch traced here: 41.7 us
  Pallas kernels  38.4 us (91%)
  local copies, waits for them, and re-layouts  2.58 us (6%)
  between operations  0.69 us (2%)
    pallas_call x1, Pallas kernels, body(): pl.pallas_call(couple_kernel, out_shape=(pltpu.VMEM((fluxes, cells), jnp....  31 us
    pallas_call x1, Pallas kernels, body(): pl.pallas_call(halo_kernel, grid=(cells // tile,), out_shape=(jax.ShapeDt...  7.4 us
    unnamed x8, local copies, waits for them, and re-layouts  2.58 us

profile of v2, /device:TPU:0, one launch (start us, length us, event | category | flops | bytes accessed | tf_op | source)
XLA Modules:
  0.0 41.7 jit_solution(8161974849406210954)
XLA Ops:
  0.6 0.0 copy-start.2
  0.6 0.0 copy-start.1
  0.7 0.0 copy-start
  0.7 1.3 %copy.14.remap_send = s32[1,5,8]{2,1,0:T(8,128)} copy(s32[1,5,8]{2,0,1:T(1,128)} %param.13) | data formatting | bytes 320 | tf_op args[1]
  2.0 1.3 %copy.15.remap_target = s32[1,5,8]{2,1,0:T(8,128)} copy(s32[1,5,8]{2,0,1:T(1,128)} %param.14) | data formatting | bytes 320 | tf_op args[2]
  3.2 31.0 %couple.1 = (f32[8,4096]{1,0:T(8,128)S(1)}, f32[2,128,4096]{2,1,0:T(8,128)S(1)}, bf16[4,256,256]{2,1,0:T(8,128)(2,1)S(1)}) custom-call(s32[1,5,8]{2,1,0:T(8,128)} %copy.14.remap_send, s32[1,5,8]{2,1,0:T(8,128)} %copy.15.remap_target, s32[1,5]{1,0:T(1,128)} %remap_counts.1, f32[2,8]{1,0:T(2,128)} %coupling.1, bf16[8,3072]{1,0:T(8,128)(2,1)} %atm.1, ...), custom_call_target="tpu_custom_call" | custom-call | tf_op jit(solution)/shard_map/couple/pallas_call | solution.py:259
  34.3 0.0 copy-done.2
  34.3 0.0 copy-done.1
  34.3 0.0 copy-done
  34.3 7.4 %halo.1 = (f32[8,4096]{1,0:T(8,128)}, f32[2,128,4096]{2,1,0:T(8,128)}) custom-call(s32[1,4]{1,0:T(1,128)S(1)} %copy-done.2, s32[1,4,2,128]{3,2,1,0:T(2,128)S(1)} %copy-done.1, s32[1,4096]{1,0:T(1,128)S(1)} %bitcast.2, bf16[4,256,256]{2,1,0:T(8,128)(2,1)S(1)} %get-tuple-element.5.received, f32[8,4096]{1,0:T(8,128)S(1)} %get-tuple-element.6.flux_in, ...), custom_call_target="tpu_custom_call" | custom-call | tf_op jit(solution)/shard_map/halo/pallas_call | solution.py:302
Async XLA Ops:
  0.6 33.6 %copy-start.2 = (s32[1,4]{1,0:T(1,128)S(1)}, s32[1,4]{1,0:T(1,128)}, u32[]{:S(2)}) copy-start(s32[1,4]{1,0:T(1,128)} %halo_rows.1) | copy-start | bytes 52
  0.6 33.6 %copy-start.1 = (s32[1,4,2,128]{3,2,1,0:T(2,128)S(1)}, s32[1,4,2,128]{3,2,1,0:T(2,128)}, u32[]{:S(2)}) copy-start(s32[1,4,2,128]{3,2,1,0:T(2,128)} %halo_ghost.1) | copy-start | bytes 12292
  0.7 33.6 %copy-start = (s32[4096]{0:T(1024)S(1)}, s32[4096]{0:T(1024)}, u32[]{:S(2)}) copy-start(s32[4096]{0:T(1024)} %param.19) | copy-start | bytes 49156

commit v3 on v2

--- a/solution.py
+++ b/solution.py
@@ -7,7 +7,7 @@
 
 MESH = pl.DeviceIdType.MESH
 CHUNKS = 8
-TILE = 1024
+TILE = 512
 
 
 def split(value):
@@ -24,15 +24,18 @@
     remap_target,
     remap_counts,
     coupling,
+    halo_rows,
     atm,
     wet,
     halo_send,
+    halo_ghost,
     weights_hbm,
     tracer_hbm,
     inverse_hbm,
     flux_out,
     mixed,
     received,
+    scatter,
     weights,
     tracer,
     inverse,
@@ -51,7 +54,7 @@
 ):
     size = lax.axis_size("patch")
     me = lax.axis_index("patch")
-    spans, slots = remap_send.shape[1], remap_send.shape[2]
+    spans, slots = remap_send.shape[0], remap_send.shape[2]
     radius = spans // 2
     tracers, levels, cells = tracer.shape
     block = weights.shape[-1]
@@ -93,7 +96,7 @@
     blank = jnp.zeros((fluxes, block), jnp.int32)
     for d in range(spans):
         for c in range(slots):
-            wanted = blank + remap_send[0, d, c]
+            wanted = blank + remap_send[d, 0, c]
             piece = sources[0]
             for a in range(1, len(sources)):
                 piece = jnp.where(wanted == a, sources[a], piece)
@@ -142,7 +145,7 @@
         for c in range(slots):
             used = (blank + remap_counts[0, d]) > c
             piece = jnp.where(used, arrived[d, c].astype(jnp.float32), 0.0)
-            placed = jnp.where(owner == remap_target[0, d, c], piece[None], 0.0)
+            placed = jnp.where(owner == remap_target[d, 0, c], piece[None], 0.0)
             pieces.append(placed.reshape(blocks * fluxes, block).astype(jnp.bfloat16))
         left = jnp.concatenate(pieces, axis=1)
         term = product(left, weights[d].reshape(slots * block, block))
@@ -162,8 +165,8 @@
 
     top = lax.broadcasted_iota(jnp.int32, (levels, block), 0) == 0
 
-    def mix_block(k, _):
-        run = pl.ds(pl.multiple_of(k * block, block), block)
+    def mix_block(k):
+        run = slice(k * block, (k + 1) * block)
         high, low = split(inverse[k])
         wetf = wet[0:1, run].astype(jnp.float32)
         held = [tracer[t, :, run] for t in range(tracers)]
@@ -182,12 +185,12 @@
             value = wetf * solved[:, t * block : (t + 1) * block] + (1.0 - wetf) * held[t]
             mixed[t, :, run] = value
             sent[t * levels : (t + 1) * levels, run] = value.astype(jnp.bfloat16)
-        return 0
 
     for chunk in range(CHUNKS):
         loads[2 * chunk].wait()
         loads[2 * chunk + 1].wait()
-        lax.fori_loop(chunk * part, (chunk + 1) * part, mix_block, 0)
+        for k in range(chunk * part, (chunk + 1) * part):
+            mix_block(k)
 
     order = sorted(range(len(steps)), key=lambda h: (-abs(steps[h]), h))
     halo_copies = []
@@ -203,30 +206,42 @@
         )
         copy.start()
         halo_copies.append(copy)
+    ghosts = []
+    line = jnp.zeros((1, lanes), jnp.int32)
+    for h in range(len(steps)):
+        for r in range(depth):
+            used = (line + halo_rows[0, h]) > r
+            ghosts.append(jnp.where(used, halo_ghost[0, h, r : r + 1, :], -1))
+    columns = jnp.transpose(jnp.concatenate(ghosts, axis=0))
+    ones = jnp.ones((16, len(ghosts) * lanes), jnp.bfloat16)
+
+    def scatter_cells(index, _):
+        base = pl.multiple_of(index * rows, rows)
+        run = pl.ds(base, rows)
+        ids = lax.broadcasted_iota(jnp.int32, (lanes, rows), 1) + base
+        pull = 0.25 * wet[0:1, run].astype(jnp.float32)
+        for i in range(len(ghosts)):
+            hit = ids == columns[:, i : i + 1]
+            scatter[i * lanes : (i + 1) * lanes, run] = jnp.where(hit, pull, 0.0).astype(
+                jnp.bfloat16
+            )
+        keep = 1.0 - product(ones, scatter[:, run])[0:1]
+        for t in range(tracers):
+            mixed[t, :, run] = keep * mixed[t, :, run]
+        return 0
+
+    lax.fori_loop(0, cells // rows, scatter_cells, 0)
     for copy in halo_copies:
         copy.wait()
 
 
-def halo_kernel(halo_rows, halo_ghost, wet, received, flux_in, mixed, flux_out, out):
+def halo_kernel(received, scatter, kept, flux_in, flux_out, out):
     tracers, levels, tile = out.shape
     run = pl.ds(pl.multiple_of(pl.program_id(0) * tile, tile), tile)
-    hosts, depth, lanes = halo_ghost.shape[1:]
-    ids = lax.broadcasted_iota(jnp.int32, (tile, lanes), 0) + pl.program_id(0) * tile
-    columns = []
-    for h in range(hosts):
-        for r in range(depth):
-            ghost = jnp.where(r < halo_rows[0, h], halo_ghost[0, h, r : r + 1, :], -1)
-            columns.append(jnp.where(ids == ghost, 1.0, 0.0).astype(jnp.bfloat16))
-    table = jnp.concatenate(columns, axis=1)
-    values = jnp.concatenate([received[h] for h in range(hosts)], axis=1)
-    contract = (((1,), (1,)), ((), ()))
-    summed = lax.dot_general(values, table, contract, preferred_element_type=jnp.float32)
-    ones = jnp.ones((16, table.shape[1]), jnp.bfloat16)
-    hits = lax.dot_general(ones, table, contract, preferred_element_type=jnp.float32)[0:1]
-    pull = 0.25 * wet[...].astype(jnp.float32)
+    values = jnp.concatenate([received[h] for h in range(received.shape[0])], axis=1)
+    summed = product(values, scatter[:, run])
     for t in range(tracers):
-        value = mixed[t, :, run]
-        out[t] = value + pull * (summed[t * levels : (t + 1) * levels] - hits * value)
+        out[t] = kept[t, :, run] + summed[t * levels : (t + 1) * levels]
     flux_out[...] = flux_in[...]
 
 
@@ -256,15 +271,16 @@
     vmem = pl.BlockSpec(memory_space=pltpu.VMEM)
     smem = pl.BlockSpec(memory_space=pltpu.SMEM)
     hbm = pl.BlockSpec(memory_space=pltpu.HBM)
-    flux, mixed, received = pl.pallas_call(
+    flux, kept, received, scatter = pl.pallas_call(
         couple_kernel,
         out_shape=(
             pltpu.VMEM((fluxes, cells), jnp.float32),
             pltpu.VMEM((tracers, levels, cells), jnp.float32),
             pltpu.VMEM((hosts, features, picks), jnp.bfloat16),
-        ),
-        in_specs=[smem] * 4 + [vmem] * 3 + [hbm] * 3,
-        out_specs=(vmem, vmem, vmem),
+            pltpu.VMEM((hosts * picks, cells), jnp.bfloat16),
+        ),
+        in_specs=[smem] * 5 + [vmem] * 4 + [hbm] * 3,
+        out_specs=(vmem, vmem, vmem, vmem),
         scratch_shapes=[
             pltpu.VMEM((spans, slots, block, block), jnp.bfloat16),
             pltpu.VMEM((tracers, levels, cells), jnp.float32),
@@ -283,17 +299,19 @@
             pltpu.SemaphoreType.DMA((hosts,)),
         ],
         compiler_params=pltpu.CompilerParams(
-            collective_id=0, has_side_effects=True, vmem_limit_bytes=58 * 1024 * 1024
+            collective_id=0, has_side_effects=True, vmem_limit_bytes=50 * 1024 * 1024 + 512 * 1024
         ),
         name="couple",
     )(
-        remap_send,
-        remap_target,
+        remap_send.transpose(1, 0, 2),
+        remap_target.transpose(1, 0, 2),
         remap_counts,
         coupling,
+        halo_rows,
         atm_flux,
         wet_row,
         halo_send,
+        halo_ghost,
         remap_weights,
         tracer,
         mix_inverse,
@@ -306,21 +324,14 @@
             jax.ShapeDtypeStruct((fluxes, cells), jnp.float32),
             jax.ShapeDtypeStruct((tracers, levels, cells), jnp.float32),
         ),
-        in_specs=[
-            smem,
-            pl.BlockSpec(memory_space=pltpu.VMEM),
-            pl.BlockSpec((1, tile), lambda i: (0, i)),
-            pl.BlockSpec(memory_space=pltpu.VMEM),
-            pl.BlockSpec((fluxes, tile), lambda i: (0, i)),
-            pl.BlockSpec(memory_space=pltpu.VMEM),
-        ],
+        in_specs=[vmem, vmem, vmem, pl.BlockSpec((fluxes, tile), lambda i: (0, i))],
         out_specs=(
             pl.BlockSpec((fluxes, tile), lambda i: (0, i)),
             pl.BlockSpec((tracers, levels, tile), lambda i: (0, 0, i)),
         ),
         compiler_params=pltpu.CompilerParams(vmem_limit_bytes=32 * 1024 * 1024),
         name="halo",
-    )(halo_rows, halo_ghost, wet_row, received, flux, mixed)
+    )(received, scatter, kept, flux)
 
 
 def solution(mesh):

time: 42 us -> 33.4 us (0.80)
  Pallas kernels: 38.4 us -> 32.6 us
  local copies, waits for them, and re-layouts: 2.58 us -> 0 us
    pallas_call x1, Pallas kernels: 31 us -> 27.2 us  [body(): pl.pallas_call(couple_kernel, out_shape=(pltpu.VMEM((fluxes, cells), jnp....]
    unnamed x8 -> x0, local copies, waits for them, and re-layouts: 2.58 us -> none
    pallas_call x1, Pallas kernels: 7.4 us -> 5.44 us  [body(): pl.pallas_call(halo_kernel, grid=(cells // tile,), out_shape=(jax.ShapeDt...]
where the time goes in v3:
time: 33.4 us; the launch traced here: 33.2 us
  Pallas kernels  32.6 us (98%)
  between operations  0.64 us (2%)
    pallas_call x1, Pallas kernels, body(): pl.pallas_call(couple_kernel, out_shape=(pltpu.VMEM((fluxes, cells), jnp....  27.2 us
    pallas_call x1, Pallas kernels, body(): pl.pallas_call(halo_kernel, grid=(cells // tile,), out_shape=(jax.ShapeDt...  5.44 us

profile of v3, /device:TPU:0, one launch (start us, length us, event | category | flops | bytes accessed | tf_op | source)
XLA Modules:
  0.0 33.2 jit_solution(11936339606056823079)
XLA Ops:
  0.6 27.2 %couple.1 = (f32[8,4096]{1,0:T(8,128)S(1)}, f32[2,128,4096]{2,1,0:T(8,128)S(1)}, bf16[4,256,256]{2,1,0:T(8,128)(2,1)S(1)}, bf16[1024,4096]{1,0:T(8,128)(2,1)S(1)}) custom-call(s32[5,1,8]{2,1,0:T(1,128)} %bitcast.4, s32[5,1,8]{2,1,0:T(1,128)} %bitcast.5, s32[1,5]{1,0:T(1,128)} %remap_counts.1, f32[2,8]{1,0:T(2,128)} %coupling.1, s32[1,4]{1,0:T(1,128)} %halo_rows.1, ...), custom_call_target="tpu_custom_call" | custom-call | tf_op jit(solution)/shard_map/couple/pallas_call | solution.py:274
  27.8 5.4 %halo.1 = (f32[8,4096]{1,0:T(8,128)}, f32[2,128,4096]{2,1,0:T(8,128)}) custom-call(bf16[4,256,256]{2,1,0:T(8,128)(2,1)S(1)} %get-tuple-element.6.received, bf16[1024,4096]{1,0:T(8,128)(2,1)S(1)} %get-tuple-element.7.scatter, f32[2,128,4096]{2,1,0:T(8,128)S(1)} %get-tuple-element.8.kept, f32[8,4096]{1,0:T(8,128)S(1)} %get-tuple-element.9.flux_in), custom_call_target="tpu_custom_call" | custom-call | tf_op jit(solution)/shard_map/halo/pallas_call | solution.py:320
